TPU v7x, 128 devices: a whole 4x4x4 slice. The times are simulated.
128 devices in a mesh: tp: 2 (over core), sp: 64 (over z, y, x).
Axes of the slice: x: 4, y: 4, z: 4, core: 2. Of those that a mesh axis runs over, the one named last changes fastest.
Arguments:
- x: bfloat16 [8, 4096], replicated
- seq_len: int32 [8], replicated
- ln_w: bfloat16 [4096], replicated
- w_q: bfloat16 [4096, 4096], P(None, 'tp')
- w_o: bfloat16 [4096, 4096], P('tp')
- w_gate: bfloat16 [4096, 12288], P(None, 'tp')
- w_up: bfloat16 [4096, 12288], P(None, 'tp')
- w_down: bfloat16 [12288, 4096], P('tp')
- k_cache: bfloat16 [8, 8, 32768, 128], P(None, 'tp', 'sp')
- v_cache: bfloat16 [8, 8, 32768, 128], P(None, 'tp', 'sp')
Outputs:
- output: bfloat16 [8, 4096], replicated
All inputs are finite; a program needn't handle non-finite values.
Results may differ from a plain program's by a relative error of at most 0.00725907.
Values sent between devices are 32-bit elements.
A program may use at most 1 GiB of HBM per device.

v0:
```python
import jax
import jax.numpy as jnp
from jax import lax
from jax.sharding import PartitionSpec as P

LN_EPS = 1e-5
NEG_BIG = -1e30


def layer_norm(x, ln_w):
    x_f32 = x.astype(jnp.float32)
    centered = x_f32 - jnp.mean(x_f32, axis=-1, keepdims=True)
    variance = jnp.mean(centered * centered, axis=-1, keepdims=True)
    return (centered * lax.rsqrt(variance + LN_EPS) * ln_w.astype(jnp.float32)).astype(jnp.bfloat16)


def project(act_in, weight):
    return jnp.dot(act_in, weight, preferred_element_type=jnp.float32)


def solution(mesh):
    cache_spec = P(None, 'tp', 'sp', None)
    col_spec = P(None, 'tp')
    row_spec = P('tp', None)

    def local_step(x, seq_len, ln_w, w_q, w_o, w_gate, w_up, w_down, k_cache, v_cache):
        n_rows, kv_local, seq_block, head_dim = k_cache.shape
        heads_local = w_q.shape[1] // head_dim
        group_size = heads_local // kv_local
        hidden = layer_norm(x, ln_w)
        query = project(hidden, w_q).astype(jnp.bfloat16).reshape(n_rows, kv_local, group_size, head_dim)
        positions = lax.axis_index('sp') * seq_block + jnp.arange(seq_block)
        is_live = (positions[None, :] <= seq_len[:, None])[:, None, None, :]
        scores = jnp.einsum('bkgd,bksd->bkgs', query, k_cache, preferred_element_type=jnp.float32) * head_dim ** -0.5
        scores = jnp.where(is_live, scores, NEG_BIG)
        block_max = jnp.max(scores, axis=-1)
        probs = jnp.where(is_live, jnp.exp(scores - block_max[..., None]), 0.0)
        block_sum = jnp.sum(probs, axis=-1)
        block_out = jnp.einsum('bkgs,bksd->bkgd', probs.astype(jnp.bfloat16), v_cache, preferred_element_type=jnp.float32)
        all_out = lax.all_gather(block_out, 'sp')
        all_max = lax.all_gather(block_max, 'sp')
        all_sum = lax.all_gather(block_sum, 'sp')
        glob_max = jnp.max(all_max, axis=0)
        rescale = jnp.exp(all_max - glob_max)
        total_sum = jnp.sum(all_sum * rescale, axis=0)
        attn_vals = jnp.sum(all_out * rescale[..., None], axis=0) / total_sum[..., None]
        attn_vals = attn_vals.reshape(n_rows, heads_local * head_dim).astype(jnp.bfloat16)
        attn_proj = lax.psum(project(attn_vals, w_o), 'tp')
        act_vals = (jax.nn.silu(project(hidden, w_gate)) * project(hidden, w_up)).astype(jnp.bfloat16)
        mlp_proj = lax.psum(project(act_vals, w_down), 'tp')
        x_out = (x.astype(jnp.float32) + attn_proj + mlp_proj).astype(jnp.bfloat16)
        return x_out

    return jax.shard_map(local_step, mesh=mesh,
                         in_specs=(P(), P(), P(), col_spec, row_spec,
                                   col_spec, col_spec, row_spec, cache_spec, cache_spec),
                         out_specs=P(), check_vma=False)
```

profile of v0, /device:TPU:1, one launch (start us, length us, event | category | flops | bytes accessed | tf_op | source)
XLA Modules:
  0.0 477.3 jit_solution(14829608311217732580)
XLA Ops:
  6.5 0.0 all-gather.5.cloned.1.call-start
  6.5 1.0 convert_reduce_fusion
  7.5 1.1 fusion.12
  8.6 0.7 convert_element_type.29
  9.3 0.0 copy-start.1
  9.3 0.0 copy-start.2
  9.3 0.9 broadcast_compare_fusion
  10.2 0.0 copy-start
  10.2 8.5 %convolution_convert_fusion = bf16[8,2048]{1,0:T(8,128)(2,1)S(1)} fusion(bf16[4096,2048]{1,0:T(8,128)(2,1)} %param.13, bf16[8,4096]{1,0:T(8,128)(2,1)} %param.10, f32[4096]{0:T(1024)S(1)} %convert_element_type.29, f32[8]{0:T(128)S(1)} %add_rsqrt_fusion, f32[8]{0:T(128)S(1)} %broadcast_multiply_fusion), kind=kOutput, calls=%fused_computation.4 | convolution fusion | flops 134397952 | bytes 16891968 | tf_op jit(solution)/shard_map/dot_general | solution.py:18
  18.7 0.0 copy-done.1
  18.7 1.3 fusion.31
  20.0 0.0 copy-done.2
  20.0 1.4 fusion.15
  21.4 0.0 all-gather.5.cloned.1.call-update
  21.4 0.0 all-reduce.3.cloned.1.call-start
  21.5 0.3 fusion.8
  21.8 157.9 %all-gather.1 = f32[512,4,4]{2,1,0:T(4,128)S(1)} all-gather(f32[8,4,4]{2,1,0:T(4,128)S(1)} %get-tuple-element.7), channel_id=3, replica_groups=mesh['tp'=2,'sp'=64] {'sp'}, dimensions={0}, use_global_device_ids=true | all-gather | bytes 33280 | tf_op jit(solution)/shard_map/all_gather | solution.py:41
  179.6 0.2 reduce_max.19
  179.9 147.8 %all-gather.2 = f32[512,4,4]{2,1,0:T(4,128)S(1)} all-gather(f32[8,4,4]{2,1,0:T(4,128)S(1)} %fusion.8), channel_id=4, replica_groups=mesh['tp'=2,'sp'=64] {'sp'}, dimensions={0}, use_global_device_ids=true | all-gather | bytes 33280 | tf_op jit(solution)/shard_map/all_gather | solution.py:42
  327.7 0.4 subtract_exponential_fusion
  328.1 0.5 multiply_reduce_fusion.1
  328.6 0.0 copy-done
  328.6 18.7 %fusion.28 = f32[8,6144]{1,0:T(8,128)S(1)} fusion(bf16[4096,6144]{1,0:T(8,128)(2,1)} %param.15, bf16[8,4096]{1,0:T(8,128)(2,1)S(1)} %copy-done, f32[4096]{0:T(1024)S(1)} %convert_element_type.29, f32[8]{0:T(128)S(1)} %add_rsqrt_fusion, f32[8]{0:T(128)S(1)} %broadcast_multiply_fusion), kind=kOutput, calls=%fused_computation.40 | convolution fusion | flops 402817024 | bytes 50610240 | tf_op jit(solution)/shard_map/dot_general | solution.py:18
  347.3 34.0 %fusion.1 = f32[8,4096]{1,0:T(8,128)} fusion(bf16[6144,4096]{1,0:T(8,128)(2,1)} %param.17, bf16[4096,6144]{1,0:T(8,128)(2,1)} %param.16, f32[8,6144]{1,0:T(8,128)S(1)} %fusion.28, bf16[8,4096]{1,0:T(8,128)(2,1)S(1)} %copy-done, f32[4096]{0:T(1024)S(1)} %convert_element_type.29, f32[8]{0:T(128)S(1)} %add_rsqrt_fusion, f32[8]{0:T(128)S(1)} %broadcast_multiply_fusion), kind=kOutput, calls=%fused_computation.2 | convolution fusion | flops 805765120 | bytes 101072960 | tf_op jit(solution)/shard_map/dot_general | solution.py:18
  381.3 0.0 all-gather.5.cloned.1.call-done
  381.3 4.4 multiply_reduce_fusion
  385.7 0.1 divide_convert_fusion
  385.9 8.7 %fusion.32 = f32[8,4096]{1,0:T(8,128)} fusion(bf16[8,2048]{1,0:T(8,128)(2,1)S(1)} %convert_element_type.34, bf16[2048,4096]{1,0:T(8,128)(2,1)} %param.14), kind=kOutput, calls=%fused_computation.42 | convolution fusion | flops 134217728 | bytes 16941056 | tf_op jit(solution)/shard_map/dot_general | solution.py:18
  394.6 0.0 all-reduce.3.cloned.1.call-update
  394.6 74.3 %all-reduce.3.cloned.1.call-done = (f32[8,4096]{1,0:T(8,128)}, f32[8,4096]{1,0:T(8,128)}) async-done(((f32[8,4096]{1,0:T(8,128)}, f32[8,4096]{1,0:T(8,128)}), (f32[8,4096]{1,0:T(8,128)}, f32[8,4096]{1,0:T(8,128)})) %all-reduce.3.cloned.1.call-update) | async-done | bytes 262160 | tf_op jit(solution)/shard_map/psum | solution.py:50
  468.9 1.6 fusion.18
  (4 shorter events, 0.0 us)
Async XLA Ops:
  6.5 374.7 %all-gather.5.cloned.1.call-start = ((), (), s32[]{:S(2)}) async-start(), calls=%async_computation | async-start | bytes 4259840 | tf_op jit(solution)/shard_map/all_gather | solution.py:40
  9.3 9.4 %copy-start.1 = (bf16[8,4,512,128]{3,2,1,0:T(8,128)(2,1)S(1)}, bf16[8,4,512,128]{3,2,1,0:T(8,128)(2,1)}, u32[]{:S(2)}) copy-start(bf16[8,4,512,128]{3,2,1,0:T(8,128)(2,1)} %param.18) | copy-start | bytes 12582916
  9.3 10.7 %copy-start.2 = (bf16[8,4,512,128]{3,2,1,0:T(8,128)(2,1)S(1)}, bf16[8,4,512,128]{3,2,1,0:T(8,128)(2,1)}, u32[]{:S(2)}) copy-start(bf16[8,4,512,128]{3,2,1,0:T(8,128)(2,1)} %param.19) | copy-start | bytes 12582916
  10.2 318.4 %copy-start = (bf16[8,4096]{1,0:T(8,128)(2,1)S(1)}, bf16[8,4096]{1,0:T(8,128)(2,1)}, u32[]{:S(2)}) copy-start(bf16[8,4096]{1,0:T(8,128)(2,1)} %param.10) | copy-start | bytes 196612
  21.4 447.4 %all-reduce.3.cloned.1.call-start = ((), (), s32[]{:S(2)}) async-start(), calls=%async_computation.1 | async-start | bytes 524288 | tf_op jit(solution)/shard_map/psum | solution.py:50
Sparse Core Ops, SparseCore 0:
  21.6 70.5 all-gather.4
  394.7 74.1 all-reduce.2
where the time goes:
time: 478 us; the launch traced here: 477 us
  blocking collectives  306 us (64%)
  waiting for transfers between devices  74.3 us (16%)
  matrix products  72.6 us (15%)
  between operations  13.4 us (3%)
  other arithmetic  11.2 us (2%)
    all_gather x1, blocking collectives, local_step(): all_max = lax.all_gather(block_max, 'sp')  158 us
    all_gather x1, blocking collectives, local_step(): all_sum = lax.all_gather(block_sum, 'sp')  148 us
    psum x1, waiting for transfers between devices, local_step(): mlp_proj = lax.psum(project(act_vals, w_down), 'tp')  74.3 us
    dot_general x4, matrix products, project(): return jnp.dot(act_in, weight, preferred_element_type=jnp.float32)  70 us
  transfers between devices with their start and end apart: 2, of which 1 were waited for; matrix products, arithmetic and copies ran while one was open for 11% of the time, Pallas kernels for 0%

commit v1 on v0

v1 whole, which is shorter than its diff:
```python
import functools

import jax
import jax.numpy as jnp
from jax import lax
from jax.experimental import pallas as pl
from jax.experimental.pallas import tpu as pltpu
from jax.sharding import PartitionSpec as P

LN_EPS = 1e-5
NEG_BIG = -1e30
MESH = pl.DeviceIdType.MESH
SIDE = 4
N_SP = SIDE ** 3
N_GROUP = 16
LANES = 128
Q_CHUNKS = 8


def coords(sp):
    return lax.div(sp, 16), lax.rem(lax.div(sp, 4), 4), lax.rem(sp, 4)


def octant(z, y, x):
    return 4 * lax.div(z, 2) + 2 * lax.div(y, 2) + lax.div(x, 2)


def corner(z, y, x):
    return 4 * lax.rem(z, 2) + 2 * lax.rem(y, 2) + lax.rem(x, 2)


def far_first(n):
    return n + lax.div(n, 2) * (5 - 2 * n)


def kernel(seq_ref, x_hbm, lnw_hbm, wq_hbm, wo_hbm, wg_hbm, wu_hbm, wd_hbm, k_hbm, v_hbm, out_ref,
           x_v, lnw_v, h_v, wq_v, k_v, v_v, wg_v, wu_v, wd_v, wo_v, q_v, part_v, row_v,
           att_send, att_recv, sum_send, sum_recv, fin,
           x_sem, wq_sem, k_sem, v_sem, wg_sem, wu_sem, wd_sem, wo_sem,
           att_ss, att_rs, sum_ss, sum_rs, fin_ss, fin_rs):
    n_rows, width = x_v.shape
    n_kv, seq_block, head_dim = k_v.shape[1:]
    n_heads = q_v.shape[0] // n_rows
    inner = wg_v.shape[1]
    o_rows = wo_v.shape[0]
    q_rows = wq_v.shape[1]
    piece = width // N_GROUP
    piece_rows = piece // LANES
    tp = lax.axis_index('tp')
    sp = lax.axis_index('sp')
    z, y, x = coords(sp)
    row = octant(z, y, x)
    hp = corner(z, y, x)
    member = hp * 2 + tp

    barrier = pltpu.get_barrier_semaphore()

    def tell(i, c):
        flat = lax.rem(sp * 2 + tp + i, 2 * N_SP)
        pl.semaphore_signal(barrier, inc=1, device_id={'tp': lax.rem(flat, 2), 'sp': lax.div(flat, 2)},
                            device_id_type=MESH)
        return c

    def wq_copy(i):
        return pltpu.make_async_copy(wq_hbm.at[pl.ds(i * q_rows, q_rows)], wq_v.at[i], wq_sem.at[i])

    def k_copy(b):
        return pltpu.make_async_copy(k_hbm.at[b], k_v.at[b], k_sem.at[b])

    def v_copy(b):
        return pltpu.make_async_copy(v_hbm.at[b], v_v.at[b], v_sem.at[b])

    up_rows = width // 8
    inner_at = pl.multiple_of(hp * inner, LANES)

    def wg_copy(i):
        at = pl.ds(i * up_rows, up_rows)
        return pltpu.make_async_copy(wg_hbm.at[at, pl.ds(inner_at, inner)], wg_v.at[at], wg_sem.at[i])

    def wu_copy(i):
        at = pl.ds(i * up_rows, up_rows)
        return pltpu.make_async_copy(wu_hbm.at[at, pl.ds(inner_at, inner)], wu_v.at[at], wu_sem.at[i])

    wd_copy = pltpu.make_async_copy(wd_hbm.at[pl.ds(inner_at, inner)], wd_v, wd_sem)
    wo_copy = pltpu.make_async_copy(wo_hbm.at[pl.ds(pl.multiple_of(hp * o_rows, o_rows), o_rows)], wo_v, wo_sem)

    x_copy = pltpu.make_async_copy(x_hbm, x_v, x_sem.at[0])
    lnw_copy = pltpu.make_async_copy(lnw_hbm, lnw_v, x_sem.at[1])
    x_copy.start()
    lnw_copy.start()
    for i in range(Q_CHUNKS):
        wq_copy(i).start()
    lax.fori_loop(1, 2 * N_SP, tell, 0)

    x_copy.wait()
    lnw_copy.wait()
    x_f32 = x_v[...].astype(jnp.float32)
    centered = x_f32 - jnp.mean(x_f32, axis=-1, keepdims=True)
    variance = jnp.mean(centered * centered, axis=-1, keepdims=True)
    hidden = centered * lax.rsqrt(variance + LN_EPS) * lnw_v[...].astype(jnp.float32)
    h_v[...] = hidden.astype(jnp.bfloat16)

    def q_step(i, acc):
        k_copy(i).start()
        v_copy(i).start()
        wq_copy(i).wait()
        at = pl.multiple_of(i * q_rows, q_rows)
        return acc + jnp.dot(h_v[:, pl.ds(at, q_rows)], wq_v[i], preferred_element_type=jnp.float32)

    query = lax.fori_loop(0, Q_CHUNKS, q_step, jnp.zeros((n_rows, n_heads * head_dim), jnp.float32))
    query = query.astype(jnp.bfloat16).astype(jnp.float32)
    for h in range(n_heads):
        q_v[h * n_rows:(h + 1) * n_rows, :] = query[:, h * head_dim:(h + 1) * head_dim]

    first_kv = lax.broadcasted_iota(jnp.int32, (8, head_dim), 0) < 4
    positions = sp * seq_block + lax.broadcasted_iota(jnp.int32, (8, seq_block), 1)

    def att_step(b, c):
        wg_copy(b).start()
        wu_copy(b).start()
        k_copy(b).wait()
        v_copy(b).wait()
        is_live = positions <= seq_ref[b]
        for j in range(n_kv // 2):
            q8 = q_v[pl.ds(j * 8 * n_rows + b, 8, stride=n_rows), :]
            zero = jnp.zeros_like(q8)
            q_wide = jnp.concatenate([jnp.where(first_kv, q8, zero), jnp.where(first_kv, zero, q8)], axis=1)
            k_wide = jnp.concatenate([k_v[b, 2 * j], k_v[b, 2 * j + 1]], axis=1)
            v_wide = jnp.concatenate([v_v[b, 2 * j], v_v[b, 2 * j + 1]], axis=1)
            scores = lax.dot_general(q_wide.astype(jnp.bfloat16), k_wide, (((1,), (1,)), ((), ())),
                                     preferred_element_type=jnp.float32) * head_dim ** -0.5
            scores = jnp.where(is_live, scores, NEG_BIG)
            block_max = jnp.max(scores, axis=-1, keepdims=True)
            probs = jnp.where(is_live, jnp.exp(scores - block_max), 0.0)
            block_sum = jnp.sum(probs, axis=-1, keepdims=True)
            wide = jnp.dot(probs.astype(jnp.bfloat16), v_wide, preferred_element_type=jnp.float32)
            any_live = block_sum > 0.0
            safe_sum = jnp.where(any_live, block_sum, 1.0)
            o8 = jnp.where(first_kv, wide[:, :head_dim], wide[:, head_dim:]) / safe_sum
            lse = jnp.where(any_live, block_max + jnp.log(safe_sum), NEG_BIG)
            lse8 = jnp.broadcast_to(lse, (8, head_dim))
            for r in range(4):
                att_send[b, j * 4 + r, 0:2, :] = o8[2 * r:2 * r + 2]
                att_send[b, j * 4 + r, 2:4, :] = lse8[2 * r:2 * r + 2]
        return c

    lax.fori_loop(0, n_rows, att_step, 0)
    wd_copy.start()
    wo_copy.start()

    pl.semaphore_wait(barrier, 2 * N_SP - 1)

    def att_exchange(i, c):
        n = N_SP - 1 - i
        dz, dy, dx = coords(n)
        pz = lax.rem(z + far_first(dz), SIDE)
        py = lax.rem(y + far_first(dy), SIDE)
        px = lax.rem(x + far_first(dx), SIDE)
        pltpu.make_async_remote_copy(
            src_ref=att_send.at[octant(pz, py, px), corner(pz, py, px)], dst_ref=att_recv.at[sp],
            send_sem=att_ss, recv_sem=att_rs,
            device_id={'tp': tp, 'sp': pz * 16 + py * 4 + px}, device_id_type=MESH).start()
        return c

    lax.fori_loop(0, N_SP - 1, att_exchange, 0)
    att_recv[sp] = att_send[row, hp]

    def up_step(i, acc):
        wg_copy(i).wait()
        wu_copy(i).wait()
        at = pl.multiple_of(i * up_rows, up_rows)
        h = h_v[:, pl.ds(at, up_rows)]
        return (acc[0] + jnp.dot(h, wg_v[pl.ds(at, up_rows), :], preferred_element_type=jnp.float32),
                acc[1] + jnp.dot(h, wu_v[pl.ds(at, up_rows), :], preferred_element_type=jnp.float32))

    start = jnp.zeros((n_rows, inner), jnp.float32)
    gate, up = lax.fori_loop(0, 8, up_step, (start, start))
    act = (gate * jax.nn.sigmoid(gate) * up).astype(jnp.bfloat16)
    wd_copy.wait()
    down_cols = width // 8

    def down_step(i, c):
        at = pl.ds(pl.multiple_of(i * down_cols, down_cols), down_cols)
        part_v[:, at] = jnp.dot(act, wd_v[:, at], preferred_element_type=jnp.float32)
        return c

    lax.fori_loop(0, 8, down_step, 0)
    wo_copy.wait()

    others = att_recv.at[pl.ds(0, N_SP - 1)]
    pltpu.make_async_copy(others, others, att_rs).wait()
    lse = att_recv[:, 2:4, :]
    weight = jnp.exp(lse - jnp.max(lse, axis=0, keepdims=True))
    attn = jnp.sum(att_recv[:, 0:2, :] * weight, axis=0) / jnp.sum(weight, axis=0)
    attn = jnp.concatenate([attn[0:1], attn[1:2]], axis=1)
    is_row = lax.broadcasted_iota(jnp.int32, (n_rows, 2 * head_dim), 0) == row
    attn = jnp.where(is_row, jnp.broadcast_to(attn, is_row.shape), 0.0).astype(jnp.bfloat16)

    is_mine = lax.broadcasted_iota(jnp.int32, (n_rows, down_cols), 0) == row

    def out_step(i, c):
        at = pl.ds(pl.multiple_of(i * down_cols, down_cols), down_cols)
        total = part_v[:, at] + jnp.dot(attn, wo_v[:, at], preferred_element_type=jnp.float32)
        row_v[:, at] = jnp.sum(jnp.where(is_mine, total, 0.0), axis=0, keepdims=True)
        return c

    lax.fori_loop(0, 8, out_step, 0)

    for m in range(N_GROUP):
        for r in range(piece_rows):
            sum_send[m, r:r + 1, :] = row_v[:, m * piece + r * LANES:m * piece + (r + 1) * LANES]

    def sum_exchange(i, c):
        n = N_GROUP - 1 - i
        ptp = lax.rem(tp + lax.rem(n, 2), 2)
        pz = 2 * lax.div(z, 2) + lax.rem(lax.rem(z, 2) + lax.div(n, 8), 2)
        py = 2 * lax.div(y, 2) + lax.rem(lax.rem(y, 2) + lax.rem(lax.div(n, 4), 2), 2)
        px = 2 * lax.div(x, 2) + lax.rem(lax.rem(x, 2) + lax.rem(lax.div(n, 2), 2), 2)
        pltpu.make_async_remote_copy(
            src_ref=sum_send.at[corner(pz, py, px) * 2 + ptp], dst_ref=sum_recv.at[member],
            send_sem=sum_ss, recv_sem=sum_rs,
            device_id={'tp': ptp, 'sp': pz * 16 + py * 4 + px}, device_id_type=MESH).start()
        return c

    lax.fori_loop(0, N_GROUP - 1, sum_exchange, 0)
    sum_recv[member] = sum_send[member]
    pieces = sum_recv.at[pl.ds(0, N_GROUP - 1)]
    pltpu.make_async_copy(pieces, pieces, sum_rs).wait()
    slot = row * N_GROUP + member
    fin[slot] = jnp.sum(sum_recv[...], axis=0)

    def fin_exchange(i, c):
        n = 2 * N_SP - 1 - i
        dz, dy, dx = coords(lax.div(n, 2))
        pz = lax.rem(z + far_first(dz), SIDE)
        py = lax.rem(y + far_first(dy), SIDE)
        px = lax.rem(x + far_first(dx), SIDE)
        pltpu.make_async_remote_copy(
            src_ref=fin.at[slot], dst_ref=fin.at[slot], send_sem=fin_ss, recv_sem=fin_rs,
            device_id={'tp': lax.rem(tp + lax.rem(n, 2), 2), 'sp': pz * 16 + py * 4 + px}, device_id_type=MESH).start()
        return c

    lax.fori_loop(0, 2 * N_SP - 1, fin_exchange, 0)
    arrived = fin.at[pl.ds(0, 2 * N_SP - 1)]
    pltpu.make_async_copy(arrived, arrived, fin_rs).wait()
    for c in range(width // LANES):
        m, r = c // piece_rows, c % piece_rows
        rows = jnp.concatenate([fin[b * N_GROUP + m, r:r + 1, :] for b in range(n_rows)], axis=0)
        at = slice(c * LANES, (c + 1) * LANES)
        out_ref[:, at] = x_v[:, at].astype(jnp.float32) + rows

    pltpu.make_async_copy(others, others, att_ss).wait()
    pltpu.make_async_copy(pieces, pieces, sum_ss).wait()
    pltpu.make_async_copy(arrived, arrived, fin_ss).wait()


def solution(mesh):
    cache_spec = P(None, 'tp', 'sp', None)
    col_spec = P(None, 'tp')
    row_spec = P('tp', None)

    def local_step(x, seq_len, ln_w, w_q, w_o, w_gate, w_up, w_down, k_cache, v_cache):
        n_rows, n_kv, seq_block, head_dim = k_cache.shape
        width = x.shape[1]
        q_width = w_q.shape[1]
        inner = w_gate.shape[1] // 8
        piece_rows = width // N_GROUP // LANES
        hbm = pl.BlockSpec(memory_space=pl.ANY)
        dma = pltpu.SemaphoreType.DMA
        total = pl.pallas_call(
            kernel,
            out_shape=jax.ShapeDtypeStruct((n_rows, width), jnp.float32),
            in_specs=[pl.BlockSpec(memory_space=pltpu.SMEM)] + [hbm] * 9,
            out_specs=pl.BlockSpec(memory_space=pltpu.VMEM),
            scratch_shapes=[
                pltpu.VMEM((n_rows, width), jnp.bfloat16),
                pltpu.VMEM((1, width), jnp.bfloat16),
                pltpu.VMEM((n_rows, width), jnp.bfloat16),
                pltpu.VMEM((Q_CHUNKS, width // Q_CHUNKS, q_width), jnp.bfloat16),
                pltpu.VMEM(k_cache.shape, jnp.bfloat16),
                pltpu.VMEM(v_cache.shape, jnp.bfloat16),
                pltpu.VMEM((width, inner), jnp.bfloat16),
                pltpu.VMEM((width, inner), jnp.bfloat16),
                pltpu.VMEM((inner, width), jnp.bfloat16),
                pltpu.VMEM((q_width // 8, width), jnp.bfloat16),
                pltpu.VMEM((n_rows * q_width // head_dim, head_dim), jnp.float32),
                pltpu.VMEM((n_rows, width), jnp.float32),
                pltpu.VMEM((1, width), jnp.float32),
                pltpu.VMEM((n_rows, 8, 4, LANES), jnp.float32),
                pltpu.VMEM((N_SP, 4, LANES), jnp.float32),
                pltpu.VMEM((N_GROUP, piece_rows, LANES), jnp.float32),
                pltpu.VMEM((N_GROUP, piece_rows, LANES), jnp.float32),
                pltpu.VMEM((2 * N_SP, piece_rows, LANES), jnp.float32),
                dma((2,)), dma((Q_CHUNKS,)), dma((8,)), dma((8,)), dma((8,)), dma((8,)), dma, dma,
                dma, dma, dma, dma, dma, dma,
            ],
            compiler_params=pltpu.CompilerParams(
                collective_id=0, has_side_effects=True, vmem_limit_bytes=60 * 1024 * 1024),
        )(seq_len, x, ln_w.reshape(1, width), w_q, w_o, w_gate, w_up, w_down, k_cache, v_cache)
        return total.astype(jnp.bfloat16)

    return jax.shard_map(local_step, mesh=mesh,
                         in_specs=(P(), P(), P(), col_spec, row_spec,
                                   col_spec, col_spec, row_spec, cache_spec, cache_spec),
                         out_specs=P(), check_vma=False)
```

time: 478 us -> 45 us (0.09)
  blocking collectives: 306 us -> 0 us
  waiting for transfers between devices: 74.3 us -> 0 us
  matrix products: 72.6 us -> 0 us
  Pallas kernels: 0 us -> 42 us
  between operations: 13.4 us -> 0.01 us
  other arithmetic: 11.2 us -> 1.54 us
    all_gather x2 -> x0, blocking collectives: 306 us -> none  [the longest x1 158 us: local_step(): all_max = lax.all_gather(block_max, 'sp')]
    psum x1 -> x0, waiting for transfers between devices: 74.3 us -> none  [local_step(): mlp_proj = lax.psum(project(act_vals, w_down), 'tp')]
    dot_general x6 -> x0, matrix products: 72.6 us -> none  [the longest x4 70 us: project(): return jnp.dot(act_in, weight, preferred_element_type=jnp.float32)]
    pallas_call x0 -> x1, Pallas kernels: none -> 42 us  [local_step(): pl.pallas_call(kernel, out_shape=jax.ShapeDtypeStruct((n_rows, width), jn...]
    reduce_sum x5 -> x0, other arithmetic: 7.25 us -> none  [the longest x1 4.43 us: local_step(): jnp.sum(all_out * rescale[..., None], axis=0) / total_sum[..., None]]
  transfers between devices with their start and end apart: 2 -> 0, of which waited for: 1 -> 0; matrix products, arithmetic and copies ran while one was open for 11% -> 0% of each run, Pallas kernels for 0% -> 0%
where the time goes in v1:
time: 45 us; the launch traced here: 44.9 us
  Pallas kernels  42 us (93%)
  other arithmetic  1.54 us (3%)
  local copies, waits for them, and re-layouts  1.31 us (3%)
    pallas_call x1, Pallas kernels, local_step(): pl.pallas_call(kernel, out_shape=jax.ShapeDtypeStruct((n_rows, width), jn...  42 us
    convert_element_type x1, other arithmetic, local_step(): return total.astype(jnp.bfloat16)  1.54 us
    reshape x1, local copies, waits for them, and re-layouts, local_step(): ln_w.reshape(1, width)  1.31 us

profile of v1, /device:TPU:1, one launch (start us, length us, event | category | flops | bytes accessed | tf_op | source)
XLA Modules:
  0.0 44.9 jit_solution(5359030268902132082)
XLA Ops:
  0.0 1.3 %reshape.3.lnw_hbm = bf16[1,4096]{1,0:T(2,128)(2,1)} reshape(bf16[4096]{0:T(1024)(128)(2,1)} %param.12) | data formatting | bytes 16384 | tf_op jit(solution)/shard_map/reshape | solution.py:299
  1.3 42.0 %shard_map.100 = f32[8,4096]{1,0:T(8,128)} custom-call(s32[8]{0:T(128)} %seq_ref.1, bf16[8,4096]{1,0:T(8,128)(2,1)} %x_hbm.1, bf16[1,4096]{1,0:T(2,128)(2,1)} %reshape.3.lnw_hbm, bf16[4096,2048]{1,0:T(8,128)(2,1)} %wq_hbm.1, bf16[2048,4096]{1,0:T(8,128)(2,1)} %wo_hbm.1, bf16[4096,6144]{1,0:T(8,128)(2,1)} %wg_hbm.1, bf16[4096,6144]{1,0:T(8,128)(2,1)} %wu_hbm.1, ...), custom_call_target="tpu_custom_call" | custom-call | tf_op jit(solution)/shard_map/pallas_call | solution.py:270
  43.3 1.5 %convert_element_type.3 = bf16[8,4096]{1,0:T(8,128)(2,1)} convert(f32[8,4096]{1,0:T(8,128)} %shard_map.100) | non-fusion elementwise | flops 32768 | bytes 196608 | tf_op jit(solution)/shard_map/convert_element_type | solution.py:300
